TPU v7x, 32 devices: a whole 2x2x4 slice. The times are simulated.
32 devices in a mesh: lat: 4 (over y, x), lon: 8 (over z, core).
Axes of the slice: x: 2, y: 2, z: 4, core: 2. Of those that a mesh axis runs over, the one named last changes fastest.
Arguments:
- ensemble: bfloat16 [32, 32, 10240], P('lon', 'lat'), may hold values from -0.625 to 0.625
- innovation: float32 [64, 64, 128], P('lon', 'lat'), may hold values from -6 to 6
- obs_weight: float32 [64, 64, 128], P('lon', 'lat'), may hold values from 0.5 to 20
- lat_offset: int32 [64], P('lat'), may hold values from 0 to 3
- lat_weight: float32 [64], P('lat'), may hold values from 0 to 1
- band_widths: int32 [80], replicated, may hold values from 1 to 63
Outputs:
- coefficients: float32 [2, 2], replicated
- next_vector: bfloat16 [32, 32, 5120], P('lon', 'lat')
All inputs are finite; a program needn't handle non-finite values.
Results may differ from a plain program's by a relative error of at most 0.0014.
Values sent between devices are 32-bit elements; how exact they have to be, the bound alone decides.
No kernel may reach another device: no remote copies, remote signals or barrier semaphores. Data moves between devices by JAX's collectives and lax.ppermute only.
A program may use at most 64 MiB of HBM per device.

v0:
```python
import jax
import jax.numpy as jnp
from jax import lax
from jax.sharding import PartitionSpec as P

M = 80
LEV = 64
FIELDS = 2
ITERS = 2
EVEN_TAPS = (-0.0234375, 0.2265625, 0.8671875, -0.0703125)
ODD_TAPS = (-0.0703125, 0.8671875, 0.2265625, -0.0234375)
EPSILON = 1e-06


def padded_2(block, sides, width, periodic):
    for axis, dim in sides:
        count = lax.axis_size(axis)
        forward = [(i, i + 1) for i in range(count - 1)]
        if periodic:
            forward.append((count - 1, 0))
        backward = [(target, source) for source, target in forward]
        low = lax.ppermute(
            lax.slice_in_dim(block, block.shape[dim] - width, None, axis=dim), axis, forward
        )
        high = lax.ppermute(lax.slice_in_dim(block, 0, width, axis=dim), axis, backward)
        block = jnp.concatenate([low, block, high], axis=dim)
    return block


def tent_matrix(band_widths, levels):
    level_ids = jnp.arange(levels, dtype=jnp.int32)
    distance = jnp.abs(level_ids[:, None] - level_ids[None, :]).astype(jnp.float32)
    widths = (band_widths + 1).astype(jnp.float32)[:, None, None]
    return jnp.maximum(0.0, 1.0 - distance[None] / widths) / widths


def tap_sum(padded, taps, first, length):
    result = taps[0] * padded[first : first + length]
    for offset in range(1, 4):
        result = result + taps[offset] * padded[first + offset : first + offset + length]
    return result


def fold_taps(padded, taps, first, length):
    result = taps[0] * padded[first : first + 2 * length : 2]
    for offset in range(1, 4):
        start_at = first - 2 * offset
        result = result + taps[offset] * padded[start_at : start_at + 2 * length : 2]
    return result


def localize(values, tent):
    lon_cols, lat_rows = (values.shape[0], values.shape[1])
    shaped = values.reshape(lon_cols, lat_rows, M, LEV)
    mapped = jnp.einsum("abml,mlk->abmk", shaped, tent, precision=lax.Precision.HIGHEST)
    return mapped.reshape(lon_cols, lat_rows, M * LEV)


def settle_rows(gathered, lat_rows):
    lon_cols, columns_all = (gathered.shape[0], gathered.shape[2])
    zeros_mid = jnp.zeros((lon_cols, lat_rows - 4, columns_all), jnp.float32)
    rim_out = jnp.concatenate([gathered[:, :2], zeros_mid, gathered[:, lat_rows + 2 :]], axis=1)
    rim_in = padded_2(rim_out, (("lat", 1),), 2, False)
    return gathered[:, 2 : lat_rows + 2] + jnp.concatenate(
        [rim_in[:, :2], zeros_mid, rim_in[:, lat_rows + 2 :]], axis=1
    )


def per_device(ensemble, innovation, obs_weight, lat_offset, lat_weight, band_widths):
    lon_cols, lat_rows = (ensemble.shape[0], ensemble.shape[1])
    fine_cols, fine_rows = (innovation.shape[0], innovation.shape[1])
    columns_all = innovation.shape[2]
    tent = tent_matrix(band_widths, LEV)
    row_ids = jnp.arange(fine_rows, dtype=jnp.int32)
    lower = row_ids // 2 + lat_offset
    columns = jnp.arange(lat_rows + 4, dtype=jnp.int32)
    interp = (1.0 - lat_weight)[:, None] * (columns[None, :] == lower[:, None]) + lat_weight[
        :, None
    ] * (columns[None, :] == lower[:, None] + 1)
    entries = float(lon_cols * lat_rows * M * LEV * lax.axis_size("lat") * lax.axis_size("lon"))
    position = lax.axis_index("lat")
    keep_rows = (
        ((columns >= 2) | (position > 0))
        & ((columns < lat_rows + 2) | (position < lax.axis_size("lat") - 1))
    ).astype(jnp.float32)

    def spread(coarse):
        shaped = ensemble.reshape(lon_cols, lat_rows, M, FIELDS, LEV)
        summed = jnp.sum(shaped * coarse.reshape(lon_cols, lat_rows, 1, FIELDS, LEV), axis=3)
        return localize(summed.reshape(lon_cols, lat_rows, M * LEV), tent)

    def restrict(fine):
        padded = padded_2(fine, (("lon", 0),), 3, True)
        coarse_lon = fold_taps(padded, EVEN_TAPS, 7, lon_cols) + fold_taps(
            padded, ODD_TAPS, 6, lon_cols
        )
        gathered = jnp.einsum("ri,crl->cil", interp, coarse_lon, precision=lax.Precision.HIGHEST)
        return settle_rows(gathered, lat_rows)

    current = spread(restrict(obs_weight * innovation))
    basis = []
    diagonal = []
    off_diagonal = []
    for step in range(ITERS):
        weights = localize(current, tent)
        combine_shaped = ensemble.reshape(lon_cols, lat_rows, M, FIELDS, LEV)
        combine_summed = jnp.sum(
            combine_shaped * weights.reshape(lon_cols, lat_rows, M, 1, LEV), axis=2
        )
        prolong_padded = padded_2(
            combine_summed.reshape(lon_cols, lat_rows, FIELDS * LEV),
            (("lat", 1), ("lon", 0)),
            2,
            True,
        )
        prolong_padded = prolong_padded * keep_rows[None, :, None]
        fine_lat = jnp.einsum(
            "ri,cil->crl", interp, prolong_padded, precision=lax.Precision.HIGHEST
        )
        even_cols = tap_sum(fine_lat, EVEN_TAPS, 0, lon_cols)
        odd_cols = tap_sum(fine_lat, ODD_TAPS, 1, lon_cols)
        image_raw = current + spread(
            restrict(
                obs_weight
                * jnp.stack([even_cols, odd_cols], axis=1).reshape(
                    fine_cols, fine_rows, columns_all
                )
            )
        )
        local_dots = jnp.stack(
            [jnp.sum(member * image_raw) for member in basis]
            + [jnp.sum(current * image_raw), jnp.sum(current * current)]
        )
        sums_all = lax.psum(local_dots, ("lat", "lon"))
        norm_value = jnp.sqrt(sums_all[-1] / entries + EPSILON)
        normed = current / norm_value
        image = image_raw / norm_value
        dots = jnp.concatenate(
            [
                sums_all[:-2] / (entries * norm_value),
                sums_all[-2:-1] / (entries * norm_value * norm_value),
            ]
        )
        basis.append(normed)
        for which_one, member in enumerate(basis):
            image = image - dots[which_one] * member
        diagonal.append(dots[-1])
        off_diagonal.append(norm_value)
        current = image
    coefficients = jnp.stack([jnp.stack(diagonal), jnp.stack(off_diagonal)])
    return (coefficients, current.astype(jnp.bfloat16))


def solution(mesh):
    return jax.shard_map(
        per_device,
        mesh=mesh,
        in_specs=(
            P("lon", "lat", None),
            P("lon", "lat", None),
            P("lon", "lat", None),
            P("lat"),
            P("lat"),
            P(),
        ),
        out_specs=(P(), P("lon", "lat", None)),
        check_vma=False,
    )
```

profile of v0, /device:TPU:10, one launch (start us, length us, event | category | flops | bytes accessed | tf_op | source)
XLA Modules:
  0.0 196.6 jit_solution(7050286283298592275)
XLA Ops:
  0.6 0.9 mul.260
  1.6 1.7 collective-permute-start.1
  3.3 0.7 add_convert_fusion
  4.0 0.7 broadcast_add_fusion
  4.6 0.7 broadcast_subtract_fusion
  5.3 0.8 convolution_bitcast_fusion.8
  6.2 3.4 %collective-permute-start.2 = (f32[4,2,128]{2,1,0:T(2,128)S(1)}, f32[4,2,128]{2,1,0:T(2,128)S(1)}, u32[]{:S(2)}, u32[]{:S(2)}) collective-permute-start(f32[4,2,128]{2,1,0:T(2,128)S(1)} %get-tuple-element.27), channel_id=1, source_target_pairs={{0,8},{8,16},{16,24},{1,9},{9,17},{17,25},{2,10},{10,18},{18,26},{... | collective-permute-start | bytes 12296 | tf_op jit(solution)/shard_map/ppermute | solution.py:22
  9.6 2.4 %collective-permute-start.3 = (f32[4,2,128]{2,1,0:T(2,128)S(1)}, f32[4,2,128]{2,1,0:T(2,128)S(1)}, u32[]{:S(2)}, u32[]{:S(2)}) collective-permute-start(f32[4,2,128]{2,1,0:T(2,128)S(1)} %get-tuple-element.28), channel_id=1, source_target_pairs={{8,0},{16,8},{24,16},{9,1},{17,9},{25,17},{10,2},{18,10},{26,18},{... | collective-permute-start | bytes 12296 | tf_op jit(solution)/shard_map/ppermute | solution.py:25
  12.1 3.5 %reshape.94 = f32[4,8,80,2,64]{4,3,2,1,0:T(2,128)S(1)} reshape(bf16[4,8,10240]{2,1,0:T(8,128)(2,1)} %param.6) | data formatting | bytes 1966080 | tf_op jit(solution)/shard_map/convert_element_type | solution.py:89
  15.6 0.4 collective-permute-done.3
  16.1 0.1 mul.273
  16.2 3.8 %multiply_reduce_fusion.4 = f32[4,8,80,64]{3,2,1,0:T(8,128)S(1)} fusion(f32[4,8,80,2,64]{4,3,2,1,0:T(2,128)S(1)} %reshape.94, f32[4,8,2,64]{3,2,1,0:T(2,128)S(1)} %mul.273), kind=kLoop, calls=%fused_computation.7 | loop fusion | flops 491520 | bytes 1982464 | tf_op jit(solution)/shard_map/reduce_sum | solution.py:89
  20.0 3.0 %fusion.8 = f32[80,64,32]{1,2,0:S(1)} fusion(f32[4,8,80,64]{3,2,1,0:T(8,128)S(1)} %multiply_reduce_fusion.4, f32[80]{0:T(128)S(1)} %add_convert_fusion, f32[64,64]{1,0:T(8,128)S(1)} %abs_convert_fusion), kind=kOutput, calls=%fused_computation.18 | convolution fusion | flops 127139840 | bytes 1327424
  23.1 2.8 %convolution_bitcast_fusion.3 = f32[4,8,80,64]{3,1,0,2:T(8,128)S(1)} fusion(f32[80,64,32]{1,2,0:S(1)} %fusion.8, f32[80]{0:T(128)S(1)} %add_convert_fusion, f32[64,64]{1,0:T(8,128)S(1)} %abs_convert_fusion), kind=kOutput, calls=%fused_computation.11 | convolution fusion | flops 127139840 | bytes 1327424
  25.9 0.8 copy.20
  26.7 2.0 multiply_reduce_fusion.3
  28.7 0.1 reshape.90
  28.8 2.1 %collective-permute-start.4 = (f32[4,2,128]{2,1,0:T(2,128)S(1)}, f32[4,2,128]{2,1,0:T(2,128)S(1)}, u32[]{:S(2)}, u32[]{:S(2)}) collective-permute-start(f32[4,2,128]{2,1,0:T(2,128)S(1)} %get-tuple-element.31), channel_id=1, source_target_pairs={{0,8},{8,16},{16,24},{24,0},{1,9},{9,17},{17,25},{25,1},{2,10},{10... | collective-permute-start | bytes 12296 | tf_op jit(solution)/shard_map/ppermute | solution.py:22
  30.8 1.6 collective-permute-done.4
  32.4 2.9 %collective-permute-done.5 = f32[4,2,128]{2,1,0:T(2,128)S(1)} collective-permute-done((f32[4,2,128]{2,1,0:T(2,128)S(1)}, f32[4,2,128]{2,1,0:T(2,128)S(1)}, u32[]{:S(2)}, u32[]{:S(2)}) %collective-permute-start.5) | collective-permute-done | bytes 4128 | tf_op jit(solution)/shard_map/ppermute | solution.py:25
  35.4 1.7 collective-permute-start.7
  37.2 1.4 collective-permute-done.6
  38.6 0.3 convolution_bitcast_fusion.5
  39.0 1.7 collective-permute-start.8
  40.7 0.1 collective-permute-start.9
  40.8 1.5 collective-permute-done.8
  42.4 0.2 convolution_bitcast_fusion.7
  42.6 1.9 collective-permute-start.10
  44.5 3.9 %collective-permute-start.11 = (f32[4,2,128]{2,1,0:T(2,128)S(1)}, f32[4,2,128]{2,1,0:T(2,128)S(1)}, u32[]{:S(2)}, u32[]{:S(2)}) collective-permute-start(f32[4,2,128]{2,1,0:T(2,128)S(1)} %get-tuple-element.24), channel_id=1, source_target_pairs={{8,0},{16,8},{24,16},{9,1},{17,9},{25,17},{10,2},{18,10},{26,18},{... | collective-permute-start | bytes 12296 | tf_op jit(solution)/shard_map/ppermute | solution.py:25
  48.4 2.5 %collective-permute-done.11 = f32[4,2,128]{2,1,0:T(2,128)S(1)} collective-permute-done((f32[4,2,128]{2,1,0:T(2,128)S(1)}, f32[4,2,128]{2,1,0:T(2,128)S(1)}, u32[]{:S(2)}, u32[]{:S(2)}) %collective-permute-start.11) | collective-permute-done | bytes 4128 | tf_op jit(solution)/shard_map/ppermute | solution.py:25
  51.0 0.1 mul.296
  51.1 3.8 %multiply_reduce_fusion.2 = f32[4,8,80,64]{3,2,1,0:T(8,128)S(1)} fusion(f32[4,8,80,2,64]{4,3,2,1,0:T(2,128)S(1)} %reshape.94, f32[4,8,2,64]{3,2,1,0:T(2,128)S(1)} %mul.296), kind=kLoop, calls=%fused_computation.5 | loop fusion | flops 491520 | bytes 1982464 | tf_op jit(solution)/shard_map/reduce_sum | solution.py:89
  54.9 4.8 %fusion.10 = (f32[]{:T(128)}, f32[]{:T(128)}, f32[4,8,80,64]{3,1,0,2:T(8,128)}) fusion(f32[80,64,32]{1,2,0:S(1)} %copy-done.1, f32[4,8,80,64]{3,2,1,0:T(8,128)S(1)} %multiply_reduce_fusion.2, f32[80]{0:T(128)S(1)} %add_convert_fusion, f32[64,64]{1,0:T(8,128)S(1)} %abs_convert_fusion), kind=kOutput, calls=%fused_computation.23 | convolution fusion | flops 127959040 | bytes 1982792
  59.7 1.4 pad_maximum_fusion.8
  61.1 45.0 %psum.14 = f32[2]{0:T(128)S(1)} all-reduce(f32[2]{0:T(128)S(1)} %pad_maximum_fusion.8), channel_id=1, replica_groups=mesh['lat'=4,'lon'=8] {'lat','lon'}, use_global_device_ids=true, to_apply=%region_5.6 | all-reduce | flops 2 | bytes 16 | tf_op jit(solution)/shard_map/psum | solution.py:134
  106.1 0.6 fusion.203
  108.0 4.7 %convolution_bitcast_fusion.1 = f32[4,8,80,64]{3,1,0,2:T(8,128)S(1)} fusion(f32[80]{0:T(128)S(1)} %add_convert_fusion, f32[64,64]{1,0:T(8,128)S(1)} %abs_convert_fusion, f32[4,8,80,64]{3,1,0,2:T(8,128)} %get-tuple-element.38, f32[]{:T(128)} %bitcast.25, f32[]{:T(128)} %bitcast.23, f32[80,64,32]{1,2,0} %copy-done), kind=kOutput, calls=%fused_computation.9 | convolution fusion | flops 127795200 | bytes 1982792
  112.8 0.8 copy.24
  113.6 1.4 multiply_reduce_fusion.1
  115.0 0.1 reshape.92
  115.1 1.5 collective-permute-start.12
  116.6 0.6 collective-permute-start.13
  117.1 1.6 collective-permute-done.12
  118.7 2.4 %collective-permute-done.13 = f32[4,2,128]{2,1,0:T(2,128)S(1)} collective-permute-done((f32[4,2,128]{2,1,0:T(2,128)S(1)}, f32[4,2,128]{2,1,0:T(2,128)S(1)}, u32[]{:S(2)}, u32[]{:S(2)}) %collective-permute-start.13) | collective-permute-done | bytes 4128 | tf_op jit(solution)/shard_map/ppermute | solution.py:25
  121.2 1.7 collective-permute-start.15
  122.9 1.4 collective-permute-done.14
  124.4 0.3 convolution_bitcast_fusion.4
  124.7 0.9 collective-permute-start.16
  125.6 0.9 collective-permute-start.17
  126.6 1.5 collective-permute-done.16
  128.1 0.2 convolution_bitcast_fusion.6
  128.3 1.9 collective-permute-start.18
  130.2 4.1 %collective-permute-start.19 = (f32[4,2,128]{2,1,0:T(2,128)S(1)}, f32[4,2,128]{2,1,0:T(2,128)S(1)}, u32[]{:S(2)}, u32[]{:S(2)}) collective-permute-start(f32[4,2,128]{2,1,0:T(2,128)S(1)} %get-tuple-element.20), channel_id=1, source_target_pairs={{8,0},{16,8},{24,16},{9,1},{17,9},{25,17},{10,2},{18,10},{26,18},{... | collective-permute-start | bytes 12296 | tf_op jit(solution)/shard_map/ppermute | solution.py:25
  134.4 2.3 %collective-permute-done.19 = f32[4,2,128]{2,1,0:T(2,128)S(1)} collective-permute-done((f32[4,2,128]{2,1,0:T(2,128)S(1)}, f32[4,2,128]{2,1,0:T(2,128)S(1)}, u32[]{:S(2)}, u32[]{:S(2)}) %collective-permute-start.19) | collective-permute-done | bytes 4128 | tf_op jit(solution)/shard_map/ppermute | solution.py:25
  136.7 0.1 mul.324
  136.8 3.8 %multiply_reduce_fusion = f32[4,8,80,64]{3,2,1,0:T(8,128)S(1)} fusion(f32[4,8,80,2,64]{4,3,2,1,0:T(2,128)S(1)} %reshape.94, f32[4,8,2,64]{3,2,1,0:T(2,128)S(1)} %mul.324), kind=kLoop, calls=%fused_computation.3 | loop fusion | flops 491520 | bytes 1982464 | tf_op jit(solution)/shard_map/reduce_sum | solution.py:89
  140.7 5.1 %multiply_reduce_fusion.7 = (f32[]{:T(128)}, f32[]{:T(128)}, f32[]{:T(128)}, f32[4,8,80,64]{3,1,0,2:T(8,128)}) fusion(f32[]{:T(128)} %bitcast.23, f32[80,64,32]{1,2,0:S(1)} %copy-done.2, f32[4,8,80,64]{3,2,1,0:T(8,128)S(1)} %multiply_reduce_fusion, f32[80]{0:T(128)S(1)} %add_convert_fusion, f32[64,64]{1,0:T(8,128)S(1)} %abs_convert_fusion, f32[]{:T(128)} %bitcast.25, ...), kind=kOutput, calls=%fused_computation.31 | convolution fusion | flops 128942080 | bytes 2638164
  145.8 2.1 %pad_maximum_fusion.9 = f32[3]{0:T(128)S(1)} fusion(f32[1]{0:T(128)} %bitcast.42, f32[1]{0:T(128)} %bitcast.41, f32[1]{0:T(128)} %bitcast.40), kind=kLoop, calls=%fused_computation.211 | loop fusion | flops 6 | bytes 24 | tf_op jit(solution)/shard_map/stack | solution.py:130
  147.9 41.9 %psum.15 = f32[3]{0:T(128)S(1)} all-reduce(f32[3]{0:T(128)S(1)} %pad_maximum_fusion.9), channel_id=1, replica_groups=mesh['lat'=4,'lon'=8] {'lat','lon'}, use_global_device_ids=true, to_apply=%region_11.12 | all-reduce | flops 3 | bytes 24 | tf_op jit(solution)/shard_map/psum | solution.py:134
  189.7 0.6 fusion.202
  192.6 1.8 subtract_convert_fusion
  194.4 0.3 copy.28
  194.6 1.2 reshape.103
  195.8 0.6 pad_maximum_fusion.7
  (60 shorter events, 1.0 us)
Async XLA Ops:
  1.5 3.8 %collective-permute-start = (f32[3,16,128]{2,1,0:T(8,128)S(1)}, f32[3,16,128]{2,1,0:T(8,128)S(1)}, u32[]{:S(2)}, u32[]{:S(2)}) collective-permute-start(f32[3,16,128]{2,1,0:T(8,128)S(1)} %get-tuple-element.17), channel_id=1, source_target_pairs={{0,1},{1,2},{2,3},{3,4},{4,5},{5,6},{6,7},{7,0},{8,9},{9,10},{10,1... | collective-permute-start | bytes 73736 | tf_op jit(solution)/shard_map/ppermute | solution.py:22
  1.6 3.7 %collective-permute-start.1 = (f32[3,16,128]{2,1,0:T(8,128)S(1)}, f32[3,16,128]{2,1,0:T(8,128)S(1)}, u32[]{:S(2)}, u32[]{:S(2)}) collective-permute-start(f32[3,16,128]{2,1,0:T(8,128)S(1)} %get-tuple-element.18), channel_id=1, source_target_pairs={{1,0},{2,1},{3,2},{4,3},{5,4},{6,5},{7,6},{0,7},{9,8},{10,9},{11,1... | collective-permute-start | bytes 73736 | tf_op jit(solution)/shard_map/ppermute | solution.py:25
  6.2 9.4 %collective-permute-start.2 = (f32[4,2,128]{2,1,0:T(2,128)S(1)}, f32[4,2,128]{2,1,0:T(2,128)S(1)}, u32[]{:S(2)}, u32[]{:S(2)}) collective-permute-start(f32[4,2,128]{2,1,0:T(2,128)S(1)} %get-tuple-element.27), channel_id=1, source_target_pairs={{0,8},{8,16},{16,24},{1,9},{9,17},{17,25},{2,10},{10,18},{18,26},{... | collective-permute-start | bytes 12296 | tf_op jit(solution)/shard_map/ppermute | solution.py:22
  9.6 6.4 %collective-permute-start.3 = (f32[4,2,128]{2,1,0:T(2,128)S(1)}, f32[4,2,128]{2,1,0:T(2,128)S(1)}, u32[]{:S(2)}, u32[]{:S(2)}) collective-permute-start(f32[4,2,128]{2,1,0:T(2,128)S(1)} %get-tuple-element.28), channel_id=1, source_target_pairs={{8,0},{16,8},{24,16},{9,1},{17,9},{25,17},{10,2},{18,10},{26,18},{... | collective-permute-start | bytes 12296 | tf_op jit(solution)/shard_map/ppermute | solution.py:25
  23.1 2.9 %copy-start = (f32[80,64,32]{1,2,0}, f32[80,64,32]{1,2,0:S(1)}, u32[]{:S(2)}) copy-start(f32[80,64,32]{1,2,0:S(1)} %fusion.8) | copy-start | bytes 1966084
  26.7 11.9 %copy-start.7 = (f32[16]{0:T(128)S(1)}, f32[16]{0:T(128)}, u32[]{:S(2)}) copy-start(f32[16]{0:T(128)} %param.10) | copy-start | bytes 196
  26.7 12.2 %copy-start.6 = (f32[8,16,128]{2,1,0:T(8,128)S(1)}, f32[8,16,128]{2,1,0:T(8,128)}, u32[]{:S(2)}) copy-start(f32[8,16,128]{2,1,0:T(8,128)} %param.8) | copy-start | bytes 196612
  28.8 3.6 %collective-permute-start.4 = (f32[4,2,128]{2,1,0:T(2,128)S(1)}, f32[4,2,128]{2,1,0:T(2,128)S(1)}, u32[]{:S(2)}, u32[]{:S(2)}) collective-permute-start(f32[4,2,128]{2,1,0:T(2,128)S(1)} %get-tuple-element.31), channel_id=1, source_target_pairs={{0,8},{8,16},{16,24},{24,0},{1,9},{9,17},{17,25},{25,1},{2,10},{10... | collective-permute-start | bytes 12296 | tf_op jit(solution)/shard_map/ppermute | solution.py:22
  30.8 4.5 %collective-permute-start.5 = (f32[4,2,128]{2,1,0:T(2,128)S(1)}, f32[4,2,128]{2,1,0:T(2,128)S(1)}, u32[]{:S(2)}, u32[]{:S(2)}) collective-permute-start(f32[4,2,128]{2,1,0:T(2,128)S(1)} %get-tuple-element.32), channel_id=1, source_target_pairs={{8,0},{16,8},{24,16},{0,24},{9,1},{17,9},{25,17},{1,25},{10,2},{18... | collective-permute-start | bytes 12296 | tf_op jit(solution)/shard_map/ppermute | solution.py:25
  35.4 3.2 %collective-permute-start.6 = (f32[2,12,128]{2,1,0:T(8,128)S(1)}, f32[2,12,128]{2,1,0:T(8,128)S(1)}, u32[]{:S(2)}, u32[]{:S(2)}) collective-permute-start(f32[2,12,128]{2,1,0:T(8,128)S(1)} %get-tuple-element.25), channel_id=1, source_target_pairs={{0,1},{1,2},{2,3},{3,4},{4,5},{5,6},{6,7},{7,0},{8,9},{9,10},{10,1... | collective-permute-start | bytes 36872 | tf_op jit(solution)/shard_map/ppermute | solution.py:22
  35.4 3.2 %collective-permute-start.7 = (f32[2,12,128]{2,1,0:T(8,128)S(1)}, f32[2,12,128]{2,1,0:T(8,128)S(1)}, u32[]{:S(2)}, u32[]{:S(2)}) collective-permute-start(f32[2,12,128]{2,1,0:T(8,128)S(1)} %get-tuple-element.26), channel_id=1, source_target_pairs={{1,0},{2,1},{3,2},{4,3},{5,4},{6,5},{7,6},{0,7},{9,8},{10,9},{11,1... | collective-permute-start | bytes 36872 | tf_op jit(solution)/shard_map/ppermute | solution.py:25
  39.0 3.3 %collective-permute-start.8 = (f32[3,16,128]{2,1,0:T(8,128)S(1)}, f32[3,16,128]{2,1,0:T(8,128)S(1)}, u32[]{:S(2)}, u32[]{:S(2)}) collective-permute-start(f32[3,16,128]{2,1,0:T(8,128)S(1)} %get-tuple-element.13), channel_id=1, source_target_pairs={{0,1},{1,2},{2,3},{3,4},{4,5},{5,6},{6,7},{7,0},{8,9},{9,10},{10,1... | collective-permute-start | bytes 73736 | tf_op jit(solution)/shard_map/ppermute | solution.py:22
  40.7 1.6 collective-permute-start.9
  42.6 5.9 %collective-permute-start.10 = (f32[4,2,128]{2,1,0:T(2,128)S(1)}, f32[4,2,128]{2,1,0:T(2,128)S(1)}, u32[]{:S(2)}, u32[]{:S(2)}) collective-permute-start(f32[4,2,128]{2,1,0:T(2,128)S(1)} %get-tuple-element.23), channel_id=1, source_target_pairs={{0,8},{8,16},{16,24},{1,9},{9,17},{17,25},{2,10},{10,18},{18,26},{... | collective-permute-start | bytes 12296 | tf_op jit(solution)/shard_map/ppermute | solution.py:22
  44.5 6.4 %collective-permute-start.11 = (f32[4,2,128]{2,1,0:T(2,128)S(1)}, f32[4,2,128]{2,1,0:T(2,128)S(1)}, u32[]{:S(2)}, u32[]{:S(2)}) collective-permute-start(f32[4,2,128]{2,1,0:T(2,128)S(1)} %get-tuple-element.24), channel_id=1, source_target_pairs={{8,0},{16,8},{24,16},{9,1},{17,9},{25,17},{10,2},{18,10},{26,18},{... | collective-permute-start | bytes 12296 | tf_op jit(solution)/shard_map/ppermute | solution.py:25
  51.1 3.9 %copy-start.1 = (f32[80,64,32]{1,2,0:S(1)}, f32[80,64,32]{1,2,0}, u32[]{:S(2)}) copy-start(f32[80,64,32]{1,2,0} %copy-done) | copy-start | bytes 1966084
  115.1 3.6 %collective-permute-start.12 = (f32[4,2,128]{2,1,0:T(2,128)S(1)}, f32[4,2,128]{2,1,0:T(2,128)S(1)}, u32[]{:S(2)}, u32[]{:S(2)}) collective-permute-start(f32[4,2,128]{2,1,0:T(2,128)S(1)} %get-tuple-element.29), channel_id=1, source_target_pairs={{0,8},{8,16},{16,24},{24,0},{1,9},{9,17},{17,25},{25,1},{2,10},{10... | collective-permute-start | bytes 12296 | tf_op jit(solution)/shard_map/ppermute | solution.py:22
  116.6 4.5 %collective-permute-start.13 = (f32[4,2,128]{2,1,0:T(2,128)S(1)}, f32[4,2,128]{2,1,0:T(2,128)S(1)}, u32[]{:S(2)}, u32[]{:S(2)}) collective-permute-start(f32[4,2,128]{2,1,0:T(2,128)S(1)} %get-tuple-element.30), channel_id=1, source_target_pairs={{8,0},{16,8},{24,16},{0,24},{9,1},{17,9},{25,17},{1,25},{10,2},{18... | collective-permute-start | bytes 12296 | tf_op jit(solution)/shard_map/ppermute | solution.py:25
  121.1 3.2 %collective-permute-start.14 = (f32[2,12,128]{2,1,0:T(8,128)S(1)}, f32[2,12,128]{2,1,0:T(8,128)S(1)}, u32[]{:S(2)}, u32[]{:S(2)}) collective-permute-start(f32[2,12,128]{2,1,0:T(8,128)S(1)} %get-tuple-element.21), channel_id=1, source_target_pairs={{0,1},{1,2},{2,3},{3,4},{4,5},{5,6},{6,7},{7,0},{8,9},{9,10},{10,1... | collective-permute-start | bytes 36872 | tf_op jit(solution)/shard_map/ppermute | solution.py:22
  121.2 3.2 %collective-permute-start.15 = (f32[2,12,128]{2,1,0:T(8,128)S(1)}, f32[2,12,128]{2,1,0:T(8,128)S(1)}, u32[]{:S(2)}, u32[]{:S(2)}) collective-permute-start(f32[2,12,128]{2,1,0:T(8,128)S(1)} %get-tuple-element.22), channel_id=1, source_target_pairs={{1,0},{2,1},{3,2},{4,3},{5,4},{6,5},{7,6},{0,7},{9,8},{10,9},{11,1... | collective-permute-start | bytes 36872 | tf_op jit(solution)/shard_map/ppermute | solution.py:25
  124.7 3.3 %collective-permute-start.16 = (f32[3,16,128]{2,1,0:T(8,128)S(1)}, f32[3,16,128]{2,1,0:T(8,128)S(1)}, u32[]{:S(2)}, u32[]{:S(2)}) collective-permute-start(f32[3,16,128]{2,1,0:T(8,128)S(1)} %get-tuple-element.9), channel_id=1, source_target_pairs={{0,1},{1,2},{2,3},{3,4},{4,5},{5,6},{6,7},{7,0},{8,9},{9,10},{10,1... | collective-permute-start | bytes 73736 | tf_op jit(solution)/shard_map/ppermute | solution.py:22
  125.6 2.5 %collective-permute-start.17 = (f32[3,16,128]{2,1,0:T(8,128)S(1)}, f32[3,16,128]{2,1,0:T(8,128)S(1)}, u32[]{:S(2)}, u32[]{:S(2)}) collective-permute-start(f32[3,16,128]{2,1,0:T(8,128)S(1)} %get-tuple-element.10), channel_id=1, source_target_pairs={{1,0},{2,1},{3,2},{4,3},{5,4},{6,5},{7,6},{0,7},{9,8},{10,9},{11,1... | collective-permute-start | bytes 73736 | tf_op jit(solution)/shard_map/ppermute | solution.py:25
  128.3 6.1 %collective-permute-start.18 = (f32[4,2,128]{2,1,0:T(2,128)S(1)}, f32[4,2,128]{2,1,0:T(2,128)S(1)}, u32[]{:S(2)}, u32[]{:S(2)}) collective-permute-start(f32[4,2,128]{2,1,0:T(2,128)S(1)} %get-tuple-element.19), channel_id=1, source_target_pairs={{0,8},{8,16},{16,24},{1,9},{9,17},{17,25},{2,10},{10,18},{18,26},{... | collective-permute-start | bytes 12296 | tf_op jit(solution)/shard_map/ppermute | solution.py:22
  130.2 6.4 %collective-permute-start.19 = (f32[4,2,128]{2,1,0:T(2,128)S(1)}, f32[4,2,128]{2,1,0:T(2,128)S(1)}, u32[]{:S(2)}, u32[]{:S(2)}) collective-permute-start(f32[4,2,128]{2,1,0:T(2,128)S(1)} %get-tuple-element.20), channel_id=1, source_target_pairs={{8,0},{16,8},{24,16},{9,1},{17,9},{25,17},{10,2},{18,10},{26,18},{... | collective-permute-start | bytes 12296 | tf_op jit(solution)/shard_map/ppermute | solution.py:25
  136.8 3.9 %copy-start.2 = (f32[80,64,32]{1,2,0:S(1)}, f32[80,64,32]{1,2,0}, u32[]{:S(2)}) copy-start(f32[80,64,32]{1,2,0} %copy-done) | copy-start | bytes 1966084
  136.8 3.9 %copy-start.4 = (f32[4,8,80,64]{3,1,0,2:T(8,128)S(1)}, f32[4,8,80,64]{3,1,0,2:T(8,128)}, u32[]{:S(2)}) copy-start(f32[4,8,80,64]{3,1,0,2:T(8,128)} %get-tuple-element.38) | copy-start | bytes 1966084
  140.7 51.9 %copy-start.3 = (f32[80,64,32]{1,2,0:S(1)}, f32[80,64,32]{1,2,0}, u32[]{:S(2)}) copy-start(f32[80,64,32]{1,2,0} %copy-done) | copy-start | bytes 1966084
  140.7 51.9 %copy-start.5 = (f32[4,8,80,64]{3,1,0,2:T(8,128)S(1)}, f32[4,8,80,64]{3,1,0,2:T(8,128)}, u32[]{:S(2)}) copy-start(f32[4,8,80,64]{3,1,0,2:T(8,128)} %get-tuple-element.38) | copy-start | bytes 1966084
where the time goes:
time: 200 us; the launch traced here: 197 us
  blocking collectives  86.9 us (43%)
  starting transfers between devices  30.9 us (15%)
  other arithmetic  24 us (12%)
  matrix products  22.2 us (11%)
  waiting for transfers between devices  19.5 us (10%)
  local copies, waits for them, and re-layouts  8.27 us (4%)
  between operations  4.78 us (2%)
    psum x2, blocking collectives, per_device(): sums_all = lax.psum(local_dots, ('lat', 'lon'))  86.9 us
    unnamed x5, matrix products  20.5 us
    ppermute x10, starting transfers between devices, padded_2(): lax.ppermute(lax.slice_in_dim(block, 0, width, axis=dim), axis, backward)  17.3 us
    ppermute x10, starting transfers between devices, padded_2(): lax.ppermute(lax.slice_in_dim(block, block.shape[dim] - width, None, axis...  13.6 us
    reduce_sum x3, other arithmetic, spread(): jnp.sum(shaped * coarse.reshape(lon_cols, lat_rows, 1, FIELDS, LEV), axis=3)  11.5 us
    ppermute x10, waiting for transfers between devices, padded_2(): lax.ppermute(lax.slice_in_dim(block, 0, width, axis=dim), axis, backward)  10.5 us
    ppermute x10, waiting for transfers between devices, padded_2(): lax.ppermute(lax.slice_in_dim(block, block.shape[dim] - width, None, axis...  8.92 us
  transfers between devices with their start and end apart: 20, of which 13 were waited for; matrix products, arithmetic and copies ran while one was open for 3% of the time, Pallas kernels for 0%

commit v1 on v0

--- a/solution.py
+++ b/solution.py
@@ -131,7 +131,9 @@
             [jnp.sum(member * image_raw) for member in basis]
             + [jnp.sum(current * image_raw), jnp.sum(current * current)]
         )
-        sums_all = lax.psum(local_dots, ("lat", "lon"))
+        sums_all = local_dots
+        for mesh_axis in ("lon", "lat"):
+            sums_all = lax.psum(sums_all, mesh_axis)
         norm_value = jnp.sqrt(sums_all[-1] / entries + EPSILON)
         normed = current / norm_value
         image = image_raw / norm_value

time: 200 us -> 173 us (0.86)
  the two profiles are of different devices: /device:TPU:10 before, /device:TPU:0 now
where the time goes in v1:
time: 173 us; the launch traced here: 170 us
  blocking collectives  48.8 us (28%)
  starting transfers between devices  42.6 us (25%)
  other arithmetic  24.3 us (14%)
  matrix products  22.2 us (13%)
  waiting for transfers between devices  19.3 us (11%)
  local copies, waits for them, and re-layouts  8.27 us (5%)
  between operations  4.63 us (3%)
    psum x4, blocking collectives, per_device(): sums_all = lax.psum(sums_all, mesh_axis)  48.8 us
    ppermute x10, starting transfers between devices, padded_2(): lax.ppermute(lax.slice_in_dim(block, 0, width, axis=dim), axis, backward)  25.2 us
    unnamed x5, matrix products  20.5 us
    ppermute x10, starting transfers between devices, padded_2(): lax.ppermute(lax.slice_in_dim(block, block.shape[dim] - width, None, axis...  17.4 us
    reduce_sum x3, other arithmetic, spread(): jnp.sum(shaped * coarse.reshape(lon_cols, lat_rows, 1, FIELDS, LEV), axis=3)  11.5 us
    ppermute x10, waiting for transfers between devices, padded_2(): lax.ppermute(lax.slice_in_dim(block, 0, width, axis=dim), axis, backward)  10.5 us
    ppermute x10, waiting for transfers between devices, padded_2(): lax.ppermute(lax.slice_in_dim(block, block.shape[dim] - width, None, axis...  8.88 us
    convert_element_type x1, local copies, waits for them, and re-layouts, spread(): shaped * coarse.reshape(lon_cols, lat_rows, 1, FIELDS, LEV)  3.48 us
  transfers between devices with their start and end apart: 20, of which 12 were waited for; matrix products, arithmetic and copies ran while one was open for 3% of the time, Pallas kernels for 0%

profile of v1, /device:TPU:0, one launch (start us, length us, event | category | flops | bytes accessed | tf_op | source)
XLA Modules:
  0.0 170.2 jit_solution(16314332300143544638)
XLA Ops:
  0.6 0.9 mul.260
  1.5 0.5 collective-permute-start
  2.1 4.1 %collective-permute-start.1 = (f32[3,16,128]{2,1,0:T(8,128)S(1)}, f32[3,16,128]{2,1,0:T(8,128)S(1)}, u32[]{:S(2)}, u32[]{:S(2)}) collective-permute-start(f32[3,16,128]{2,1,0:T(8,128)S(1)} %get-tuple-element.18), channel_id=1, source_target_pairs={{1,0},{2,1},{3,2},{4,3},{5,4},{6,5},{7,6},{0,7},{9,8},{10,9},{11,1... | collective-permute-start | bytes 73736 | tf_op jit(solution)/shard_map/ppermute | solution.py:25
  6.2 0.7 add_convert_fusion
  6.8 0.7 broadcast_add_fusion
  7.5 0.7 broadcast_subtract_fusion
  8.2 0.8 convolution_bitcast_fusion.8
  9.0 3.8 %collective-permute-start.2 = (f32[4,2,128]{2,1,0:T(2,128)S(1)}, f32[4,2,128]{2,1,0:T(2,128)S(1)}, u32[]{:S(2)}, u32[]{:S(2)}) collective-permute-start(f32[4,2,128]{2,1,0:T(2,128)S(1)} %get-tuple-element.27), channel_id=1, source_target_pairs={{0,8},{8,16},{16,24},{1,9},{9,17},{17,25},{2,10},{10,18},{18,26},{... | collective-permute-start | bytes 12296 | tf_op jit(solution)/shard_map/ppermute | solution.py:22
  12.9 1.3 collective-permute-start.3
  14.2 3.5 %reshape.94 = f32[4,8,80,2,64]{4,3,2,1,0:T(2,128)S(1)} reshape(bf16[4,8,10240]{2,1,0:T(8,128)(2,1)} %param.6) | data formatting | bytes 1966080 | tf_op jit(solution)/shard_map/convert_element_type | solution.py:89
  17.8 0.6 collective-permute-done.3
  18.4 0.1 mul.273
  18.5 3.8 %multiply_reduce_fusion.4 = f32[4,8,80,64]{3,2,1,0:T(8,128)S(1)} fusion(f32[4,8,80,2,64]{4,3,2,1,0:T(2,128)S(1)} %reshape.94, f32[4,8,2,64]{3,2,1,0:T(2,128)S(1)} %mul.273), kind=kLoop, calls=%fused_computation.7 | loop fusion | flops 491520 | bytes 1982464 | tf_op jit(solution)/shard_map/reduce_sum | solution.py:89
  22.4 3.0 %fusion.8 = f32[80,64,32]{1,2,0:S(1)} fusion(f32[4,8,80,64]{3,2,1,0:T(8,128)S(1)} %multiply_reduce_fusion.4, f32[80]{0:T(128)S(1)} %add_convert_fusion, f32[64,64]{1,0:T(8,128)S(1)} %abs_convert_fusion), kind=kOutput, calls=%fused_computation.18 | convolution fusion | flops 127139840 | bytes 1327424
  25.4 2.8 %convolution_bitcast_fusion.3 = f32[4,8,80,64]{3,1,0,2:T(8,128)S(1)} fusion(f32[80,64,32]{1,2,0:S(1)} %fusion.8, f32[80]{0:T(128)S(1)} %add_convert_fusion, f32[64,64]{1,0:T(8,128)S(1)} %abs_convert_fusion), kind=kOutput, calls=%fused_computation.11 | convolution fusion | flops 127139840 | bytes 1327424
  28.3 0.8 copy.20
  29.1 2.0 %multiply_reduce_fusion.3 = f32[4,8,2,64]{3,2,1,0:T(2,128)S(1)} fusion(f32[4,8,80,2,64]{4,3,2,1,0:T(2,128)S(1)} %reshape.94, f32[4,8,80,64]{3,2,1,0:T(8,128)S(1)} %copy.20), kind=kLoop, calls=%fused_computation.6 | loop fusion | flops 651264 | bytes 1982464 | tf_op jit(solution)/shard_map/reduce_sum | solution.py:107
  31.0 0.1 reshape.90
  31.1 2.4 %collective-permute-start.4 = (f32[4,2,128]{2,1,0:T(2,128)S(1)}, f32[4,2,128]{2,1,0:T(2,128)S(1)}, u32[]{:S(2)}, u32[]{:S(2)}) collective-permute-start(f32[4,2,128]{2,1,0:T(2,128)S(1)} %get-tuple-element.31), channel_id=1, source_target_pairs={{0,8},{8,16},{16,24},{24,0},{1,9},{9,17},{17,25},{25,1},{2,10},{10... | collective-permute-start | bytes 12296 | tf_op jit(solution)/shard_map/ppermute | solution.py:22
  33.6 0.7 collective-permute-start.5
  34.2 1.5 collective-permute-done.4
  35.7 1.5 collective-permute-done.5
  37.3 3.5 %collective-permute-start.7 = (f32[2,12,128]{2,1,0:T(8,128)S(1)}, f32[2,12,128]{2,1,0:T(8,128)S(1)}, u32[]{:S(2)}, u32[]{:S(2)}) collective-permute-start(f32[2,12,128]{2,1,0:T(8,128)S(1)} %get-tuple-element.26), channel_id=1, source_target_pairs={{1,0},{2,1},{3,2},{4,3},{5,4},{6,5},{7,6},{0,7},{9,8},{10,9},{11,1... | collective-permute-start | bytes 36872 | tf_op jit(solution)/shard_map/ppermute | solution.py:25
  40.9 1.4 collective-permute-done.6
  42.3 0.3 convolution_bitcast_fusion.5
  42.7 3.6 %collective-permute-start.9 = (f32[3,16,128]{2,1,0:T(8,128)S(1)}, f32[3,16,128]{2,1,0:T(8,128)S(1)}, u32[]{:S(2)}, u32[]{:S(2)}) collective-permute-start(f32[3,16,128]{2,1,0:T(8,128)S(1)} %get-tuple-element.14), channel_id=1, source_target_pairs={{1,0},{2,1},{3,2},{4,3},{5,4},{6,5},{7,6},{0,7},{9,8},{10,9},{11,1... | collective-permute-start | bytes 73736 | tf_op jit(solution)/shard_map/ppermute | solution.py:25
  46.3 1.5 collective-permute-done.8
  47.8 0.2 convolution_bitcast_fusion.7
  48.0 4.8 %collective-permute-start.10 = (f32[4,2,128]{2,1,0:T(2,128)S(1)}, f32[4,2,128]{2,1,0:T(2,128)S(1)}, u32[]{:S(2)}, u32[]{:S(2)}) collective-permute-start(f32[4,2,128]{2,1,0:T(2,128)S(1)} %get-tuple-element.23), channel_id=1, source_target_pairs={{0,8},{8,16},{16,24},{1,9},{9,17},{17,25},{2,10},{10,18},{18,26},{... | collective-permute-start | bytes 12296 | tf_op jit(solution)/shard_map/ppermute | solution.py:22
  52.8 1.3 collective-permute-start.11
  54.1 4.2 %collective-permute-done.11 = f32[4,2,128]{2,1,0:T(2,128)S(1)} collective-permute-done((f32[4,2,128]{2,1,0:T(2,128)S(1)}, f32[4,2,128]{2,1,0:T(2,128)S(1)}, u32[]{:S(2)}, u32[]{:S(2)}) %collective-permute-start.11) | collective-permute-done | bytes 4128 | tf_op jit(solution)/shard_map/ppermute | solution.py:25
  58.4 0.1 mul.296
  58.5 3.8 %multiply_reduce_fusion.2 = f32[4,8,80,64]{3,2,1,0:T(8,128)S(1)} fusion(f32[4,8,80,2,64]{4,3,2,1,0:T(2,128)S(1)} %reshape.94, f32[4,8,2,64]{3,2,1,0:T(2,128)S(1)} %mul.296), kind=kLoop, calls=%fused_computation.5 | loop fusion | flops 491520 | bytes 1982464 | tf_op jit(solution)/shard_map/reduce_sum | solution.py:89
  62.4 4.8 %fusion.10 = (f32[]{:T(128)}, f32[]{:T(128)}, f32[4,8,80,64]{3,1,0,2:T(8,128)}) fusion(f32[80,64,32]{1,2,0:S(1)} %copy-done.1, f32[4,8,80,64]{3,2,1,0:T(8,128)S(1)} %multiply_reduce_fusion.2, f32[80]{0:T(128)S(1)} %add_convert_fusion, f32[64,64]{1,0:T(8,128)S(1)} %abs_convert_fusion), kind=kOutput, calls=%fused_computation.23 | convolution fusion | flops 127959040 | bytes 1982792
  67.2 1.4 pad_maximum_fusion.8
  68.5 15.7 %psum.28 = f32[2]{0:T(128)S(1)} all-reduce(f32[2]{0:T(128)S(1)} %pad_maximum_fusion.8), channel_id=1, replica_groups=mesh['lat'=4,'lon'=8] {'lon'}, use_global_device_ids=true, to_apply=%region_5.6 | all-reduce | flops 2 | bytes 16 | tf_op jit(solution)/shard_map/psum | solution.py:136
  84.2 8.8 %psum.29 = f32[2]{0:T(128)S(1)} all-reduce(f32[2]{0:T(128)S(1)} %psum.28), channel_id=1, replica_groups=mesh['lat'=4,'lon'=8] {'lat'}, use_global_device_ids=true, to_apply=%region_6.7 | all-reduce | flops 2 | bytes 16 | tf_op jit(solution)/shard_map/psum | solution.py:136
  93.0 0.6 fusion.203
  94.9 4.7 %convolution_bitcast_fusion.1 = f32[4,8,80,64]{3,1,0,2:T(8,128)S(1)} fusion(f32[80]{0:T(128)S(1)} %add_convert_fusion, f32[64,64]{1,0:T(8,128)S(1)} %abs_convert_fusion, f32[4,8,80,64]{3,1,0,2:T(8,128)} %get-tuple-element.38, f32[]{:T(128)} %bitcast.25, f32[]{:T(128)} %bitcast.23, f32[80,64,32]{1,2,0} %copy-done), kind=kOutput, calls=%fused_computation.9 | convolution fusion | flops 127795200 | bytes 1982792
  99.7 0.8 copy.24
  100.4 1.4 multiply_reduce_fusion.1
  102.0 0.8 collective-permute-start.12
  102.8 2.1 %collective-permute-start.13 = (f32[4,2,128]{2,1,0:T(2,128)S(1)}, f32[4,2,128]{2,1,0:T(2,128)S(1)}, u32[]{:S(2)}, u32[]{:S(2)}) collective-permute-start(f32[4,2,128]{2,1,0:T(2,128)S(1)} %get-tuple-element.30), channel_id=1, source_target_pairs={{8,0},{16,8},{24,16},{0,24},{9,1},{17,9},{25,17},{1,25},{10,2},{18... | collective-permute-start | bytes 12296 | tf_op jit(solution)/shard_map/ppermute | solution.py:25
  104.9 1.6 collective-permute-done.12
  106.7 3.5 %collective-permute-start.15 = (f32[2,12,128]{2,1,0:T(8,128)S(1)}, f32[2,12,128]{2,1,0:T(8,128)S(1)}, u32[]{:S(2)}, u32[]{:S(2)}) collective-permute-start(f32[2,12,128]{2,1,0:T(8,128)S(1)} %get-tuple-element.22), channel_id=1, source_target_pairs={{1,0},{2,1},{3,2},{4,3},{5,4},{6,5},{7,6},{0,7},{9,8},{10,9},{11,1... | collective-permute-start | bytes 36872 | tf_op jit(solution)/shard_map/ppermute | solution.py:25
  110.2 1.4 collective-permute-done.14
  111.6 0.3 convolution_bitcast_fusion.4
  112.1 3.6 %collective-permute-start.17 = (f32[3,16,128]{2,1,0:T(8,128)S(1)}, f32[3,16,128]{2,1,0:T(8,128)S(1)}, u32[]{:S(2)}, u32[]{:S(2)}) collective-permute-start(f32[3,16,128]{2,1,0:T(8,128)S(1)} %get-tuple-element.10), channel_id=1, source_target_pairs={{1,0},{2,1},{3,2},{4,3},{5,4},{6,5},{7,6},{0,7},{9,8},{10,9},{11,1... | collective-permute-start | bytes 73736 | tf_op jit(solution)/shard_map/ppermute | solution.py:25
  115.6 1.5 collective-permute-done.16
  117.2 0.2 convolution_bitcast_fusion.6
  117.4 4.8 %collective-permute-start.18 = (f32[4,2,128]{2,1,0:T(2,128)S(1)}, f32[4,2,128]{2,1,0:T(2,128)S(1)}, u32[]{:S(2)}, u32[]{:S(2)}) collective-permute-start(f32[4,2,128]{2,1,0:T(2,128)S(1)} %get-tuple-element.19), channel_id=1, source_target_pairs={{0,8},{8,16},{16,24},{1,9},{9,17},{17,25},{2,10},{10,18},{18,26},{... | collective-permute-start | bytes 12296 | tf_op jit(solution)/shard_map/ppermute | solution.py:22
  122.2 1.5 collective-permute-start.19
  123.7 4.0 %collective-permute-done.19 = f32[4,2,128]{2,1,0:T(2,128)S(1)} collective-permute-done((f32[4,2,128]{2,1,0:T(2,128)S(1)}, f32[4,2,128]{2,1,0:T(2,128)S(1)}, u32[]{:S(2)}, u32[]{:S(2)}) %collective-permute-start.19) | collective-permute-done | bytes 4128 | tf_op jit(solution)/shard_map/ppermute | solution.py:25
  127.7 0.1 mul.324
  127.8 3.8 %multiply_reduce_fusion = f32[4,8,80,64]{3,2,1,0:T(8,128)S(1)} fusion(f32[4,8,80,2,64]{4,3,2,1,0:T(2,128)S(1)} %reshape.94, f32[4,8,2,64]{3,2,1,0:T(2,128)S(1)} %mul.324), kind=kLoop, calls=%fused_computation.3 | loop fusion | flops 491520 | bytes 1982464 | tf_op jit(solution)/shard_map/reduce_sum | solution.py:89
  131.7 5.1 %multiply_reduce_fusion.7 = (f32[]{:T(128)}, f32[]{:T(128)}, f32[]{:T(128)}, f32[4,8,80,64]{3,1,0,2:T(8,128)}) fusion(f32[]{:T(128)} %bitcast.23, f32[80,64,32]{1,2,0:S(1)} %copy-done.2, f32[4,8,80,64]{3,2,1,0:T(8,128)S(1)} %multiply_reduce_fusion, f32[80]{0:T(128)S(1)} %add_convert_fusion, f32[64,64]{1,0:T(8,128)S(1)} %abs_convert_fusion, f32[]{:T(128)} %bitcast.25, ...), kind=kOutput, calls=%fused_computation.31 | convolution fusion | flops 128942080 | bytes 2638164
  136.8 1.9 %pad_maximum_fusion.9 = f32[3]{0:T(128)S(1)} fusion(f32[1]{0:T(128)} %bitcast.42, f32[1]{0:T(128)} %bitcast.41, f32[1]{0:T(128)} %bitcast.40), kind=kLoop, calls=%fused_computation.211 | loop fusion | flops 6 | bytes 24 | tf_op jit(solution)/shard_map/stack | solution.py:130
  138.8 15.7 %psum.30 = f32[3]{0:T(128)S(1)} all-reduce(f32[3]{0:T(128)S(1)} %pad_maximum_fusion.9), channel_id=1, replica_groups=mesh['lat'=4,'lon'=8] {'lon'}, use_global_device_ids=true, to_apply=%region_12.13 | all-reduce | flops 3 | bytes 24 | tf_op jit(solution)/shard_map/psum | solution.py:136
  154.4 8.6 %psum.31 = f32[3]{0:T(128)S(1)} all-reduce(f32[3]{0:T(128)S(1)} %psum.30), channel_id=1, replica_groups=mesh['lat'=4,'lon'=8] {'lat'}, use_global_device_ids=true, to_apply=%region_13.14 | all-reduce | flops 3 | bytes 24 | tf_op jit(solution)/shard_map/psum | solution.py:136
  163.1 0.6 fusion.202
  165.7 2.2 %subtract_convert_fusion = bf16[4,8,80,64]{3,1,0,2:T(8,128)(2,1)S(1)} fusion(f32[4,8,80,64]{3,1,0,2:T(8,128)} %get-tuple-element.39, f32[]{:T(128)} %bitcast.49, f32[]{:T(128)} %bitcast.43, f32[]{:T(128)} %bitcast.48, f32[]{:T(128)} %bitcast.23, f32[80,64,32]{1,2,0:S(1)} %copy-done.3, f32[]{:T(128)} %bitcast.25, f32[4,8,80,64]{3,1,0,2:T(8,128)} %get-tuple-element.38), kind=kLoop, calls=%fused_computation.28 | loop fusion | flops 1802240 | bytes 2293780 | tf_op jit(solution)/shard_map/convert_element_type | solution.py:153
  167.9 0.3 copy.28
  168.2 1.2 reshape.103
  169.4 0.6 pad_maximum_fusion.7
  (60 shorter events, 1.2 us)
Async XLA Ops:
  1.5 6.6 %collective-permute-start = (f32[3,16,128]{2,1,0:T(8,128)S(1)}, f32[3,16,128]{2,1,0:T(8,128)S(1)}, u32[]{:S(2)}, u32[]{:S(2)}) collective-permute-start(f32[3,16,128]{2,1,0:T(8,128)S(1)} %get-tuple-element.17), channel_id=1, source_target_pairs={{0,1},{1,2},{2,3},{3,4},{4,5},{5,6},{6,7},{7,0},{8,9},{9,10},{10,1... | collective-permute-start | bytes 73736 | tf_op jit(solution)/shard_map/ppermute | solution.py:22
  2.1 6.1 %collective-permute-start.1 = (f32[3,16,128]{2,1,0:T(8,128)S(1)}, f32[3,16,128]{2,1,0:T(8,128)S(1)}, u32[]{:S(2)}, u32[]{:S(2)}) collective-permute-start(f32[3,16,128]{2,1,0:T(8,128)S(1)} %get-tuple-element.18), channel_id=1, source_target_pairs={{1,0},{2,1},{3,2},{4,3},{5,4},{6,5},{7,6},{0,7},{9,8},{10,9},{11,1... | collective-permute-start | bytes 73736 | tf_op jit(solution)/shard_map/ppermute | solution.py:25
  9.0 8.7 %collective-permute-start.2 = (f32[4,2,128]{2,1,0:T(2,128)S(1)}, f32[4,2,128]{2,1,0:T(2,128)S(1)}, u32[]{:S(2)}, u32[]{:S(2)}) collective-permute-start(f32[4,2,128]{2,1,0:T(2,128)S(1)} %get-tuple-element.27), channel_id=1, source_target_pairs={{0,8},{8,16},{16,24},{1,9},{9,17},{17,25},{2,10},{10,18},{18,26},{... | collective-permute-start | bytes 12296 | tf_op jit(solution)/shard_map/ppermute | solution.py:22
  12.9 5.5 %collective-permute-start.3 = (f32[4,2,128]{2,1,0:T(2,128)S(1)}, f32[4,2,128]{2,1,0:T(2,128)S(1)}, u32[]{:S(2)}, u32[]{:S(2)}) collective-permute-start(f32[4,2,128]{2,1,0:T(2,128)S(1)} %get-tuple-element.28), channel_id=1, source_target_pairs={{8,0},{16,8},{24,16},{9,1},{17,9},{25,17},{10,2},{18,10},{26,18},{... | collective-permute-start | bytes 12296 | tf_op jit(solution)/shard_map/ppermute | solution.py:25
  25.4 2.9 %copy-start = (f32[80,64,32]{1,2,0}, f32[80,64,32]{1,2,0:S(1)}, u32[]{:S(2)}) copy-start(f32[80,64,32]{1,2,0:S(1)} %fusion.8) | copy-start | bytes 1966084
  29.0 13.2 %copy-start.6 = (f32[16]{0:T(128)S(1)}, f32[16]{0:T(128)}, u32[]{:S(2)}) copy-start(f32[16]{0:T(128)} %param.10) | copy-start | bytes 196
  29.1 13.6 %copy-start.5 = (f32[8,16,128]{2,1,0:T(8,128)S(1)}, f32[8,16,128]{2,1,0:T(8,128)}, u32[]{:S(2)}) copy-start(f32[8,16,128]{2,1,0:T(8,128)} %param.8) | copy-start | bytes 196612
  31.1 4.6 %collective-permute-start.4 = (f32[4,2,128]{2,1,0:T(2,128)S(1)}, f32[4,2,128]{2,1,0:T(2,128)S(1)}, u32[]{:S(2)}, u32[]{:S(2)}) collective-permute-start(f32[4,2,128]{2,1,0:T(2,128)S(1)} %get-tuple-element.31), channel_id=1, source_target_pairs={{0,8},{8,16},{16,24},{24,0},{1,9},{9,17},{17,25},{25,1},{2,10},{10... | collective-permute-start | bytes 12296 | tf_op jit(solution)/shard_map/ppermute | solution.py:22
  33.6 3.7 %collective-permute-start.5 = (f32[4,2,128]{2,1,0:T(2,128)S(1)}, f32[4,2,128]{2,1,0:T(2,128)S(1)}, u32[]{:S(2)}, u32[]{:S(2)}) collective-permute-start(f32[4,2,128]{2,1,0:T(2,128)S(1)} %get-tuple-element.32), channel_id=1, source_target_pairs={{8,0},{16,8},{24,16},{0,24},{9,1},{17,9},{25,17},{1,25},{10,2},{18... | collective-permute-start | bytes 12296 | tf_op jit(solution)/shard_map/ppermute | solution.py:25
  37.3 5.0 %collective-permute-start.6 = (f32[2,12,128]{2,1,0:T(8,128)S(1)}, f32[2,12,128]{2,1,0:T(8,128)S(1)}, u32[]{:S(2)}, u32[]{:S(2)}) collective-permute-start(f32[2,12,128]{2,1,0:T(8,128)S(1)} %get-tuple-element.25), channel_id=1, source_target_pairs={{0,1},{1,2},{2,3},{3,4},{4,5},{5,6},{6,7},{7,0},{8,9},{9,10},{10,1... | collective-permute-start | bytes 36872 | tf_op jit(solution)/shard_map/ppermute | solution.py:22
  37.3 5.0 %collective-permute-start.7 = (f32[2,12,128]{2,1,0:T(8,128)S(1)}, f32[2,12,128]{2,1,0:T(8,128)S(1)}, u32[]{:S(2)}, u32[]{:S(2)}) collective-permute-start(f32[2,12,128]{2,1,0:T(8,128)S(1)} %get-tuple-element.26), channel_id=1, source_target_pairs={{1,0},{2,1},{3,2},{4,3},{5,4},{6,5},{7,6},{0,7},{9,8},{10,9},{11,1... | collective-permute-start | bytes 36872 | tf_op jit(solution)/shard_map/ppermute | solution.py:25
  42.7 5.1 %collective-permute-start.8 = (f32[3,16,128]{2,1,0:T(8,128)S(1)}, f32[3,16,128]{2,1,0:T(8,128)S(1)}, u32[]{:S(2)}, u32[]{:S(2)}) collective-permute-start(f32[3,16,128]{2,1,0:T(8,128)S(1)} %get-tuple-element.13), channel_id=1, source_target_pairs={{0,1},{1,2},{2,3},{3,4},{4,5},{5,6},{6,7},{7,0},{8,9},{9,10},{10,1... | collective-permute-start | bytes 73736 | tf_op jit(solution)/shard_map/ppermute | solution.py:22
  42.7 5.1 %collective-permute-start.9 = (f32[3,16,128]{2,1,0:T(8,128)S(1)}, f32[3,16,128]{2,1,0:T(8,128)S(1)}, u32[]{:S(2)}, u32[]{:S(2)}) collective-permute-start(f32[3,16,128]{2,1,0:T(8,128)S(1)} %get-tuple-element.14), channel_id=1, source_target_pairs={{1,0},{2,1},{3,2},{4,3},{5,4},{6,5},{7,6},{0,7},{9,8},{10,9},{11,1... | collective-permute-start | bytes 73736 | tf_op jit(solution)/shard_map/ppermute | solution.py:25
  48.0 6.1 %collective-permute-start.10 = (f32[4,2,128]{2,1,0:T(2,128)S(1)}, f32[4,2,128]{2,1,0:T(2,128)S(1)}, u32[]{:S(2)}, u32[]{:S(2)}) collective-permute-start(f32[4,2,128]{2,1,0:T(2,128)S(1)} %get-tuple-element.23), channel_id=1, source_target_pairs={{0,8},{8,16},{16,24},{1,9},{9,17},{17,25},{2,10},{10,18},{18,26},{... | collective-permute-start | bytes 12296 | tf_op jit(solution)/shard_map/ppermute | solution.py:22
  52.8 5.5 %collective-permute-start.11 = (f32[4,2,128]{2,1,0:T(2,128)S(1)}, f32[4,2,128]{2,1,0:T(2,128)S(1)}, u32[]{:S(2)}, u32[]{:S(2)}) collective-permute-start(f32[4,2,128]{2,1,0:T(2,128)S(1)} %get-tuple-element.24), channel_id=1, source_target_pairs={{8,0},{16,8},{24,16},{9,1},{17,9},{25,17},{10,2},{18,10},{26,18},{... | collective-permute-start | bytes 12296 | tf_op jit(solution)/shard_map/ppermute | solution.py:25
  58.5 3.9 %copy-start.1 = (f32[80,64,32]{1,2,0:S(1)}, f32[80,64,32]{1,2,0}, u32[]{:S(2)}) copy-start(f32[80,64,32]{1,2,0} %copy-done) | copy-start | bytes 1966084
  102.0 4.5 %collective-permute-start.12 = (f32[4,2,128]{2,1,0:T(2,128)S(1)}, f32[4,2,128]{2,1,0:T(2,128)S(1)}, u32[]{:S(2)}, u32[]{:S(2)}) collective-permute-start(f32[4,2,128]{2,1,0:T(2,128)S(1)} %get-tuple-element.29), channel_id=1, source_target_pairs={{0,8},{8,16},{16,24},{24,0},{1,9},{9,17},{17,25},{25,1},{2,10},{10... | collective-permute-start | bytes 12296 | tf_op jit(solution)/shard_map/ppermute | solution.py:22
  102.8 3.8 %collective-permute-start.13 = (f32[4,2,128]{2,1,0:T(2,128)S(1)}, f32[4,2,128]{2,1,0:T(2,128)S(1)}, u32[]{:S(2)}, u32[]{:S(2)}) collective-permute-start(f32[4,2,128]{2,1,0:T(2,128)S(1)} %get-tuple-element.30), channel_id=1, source_target_pairs={{8,0},{16,8},{24,16},{0,24},{9,1},{17,9},{25,17},{1,25},{10,2},{18... | collective-permute-start | bytes 12296 | tf_op jit(solution)/shard_map/ppermute | solution.py:25
  106.6 5.0 %collective-permute-start.14 = (f32[2,12,128]{2,1,0:T(8,128)S(1)}, f32[2,12,128]{2,1,0:T(8,128)S(1)}, u32[]{:S(2)}, u32[]{:S(2)}) collective-permute-start(f32[2,12,128]{2,1,0:T(8,128)S(1)} %get-tuple-element.21), channel_id=1, source_target_pairs={{0,1},{1,2},{2,3},{3,4},{4,5},{5,6},{6,7},{7,0},{8,9},{9,10},{10,1... | collective-permute-start | bytes 36872 | tf_op jit(solution)/shard_map/ppermute | solution.py:22
  106.7 5.0 %collective-permute-start.15 = (f32[2,12,128]{2,1,0:T(8,128)S(1)}, f32[2,12,128]{2,1,0:T(8,128)S(1)}, u32[]{:S(2)}, u32[]{:S(2)}) collective-permute-start(f32[2,12,128]{2,1,0:T(8,128)S(1)} %get-tuple-element.22), channel_id=1, source_target_pairs={{1,0},{2,1},{3,2},{4,3},{5,4},{6,5},{7,6},{0,7},{9,8},{10,9},{11,1... | collective-permute-start | bytes 36872 | tf_op jit(solution)/shard_map/ppermute | solution.py:25
  112.0 5.1 %collective-permute-start.16 = (f32[3,16,128]{2,1,0:T(8,128)S(1)}, f32[3,16,128]{2,1,0:T(8,128)S(1)}, u32[]{:S(2)}, u32[]{:S(2)}) collective-permute-start(f32[3,16,128]{2,1,0:T(8,128)S(1)} %get-tuple-element.9), channel_id=1, source_target_pairs={{0,1},{1,2},{2,3},{3,4},{4,5},{5,6},{6,7},{7,0},{8,9},{9,10},{10,1... | collective-permute-start | bytes 73736 | tf_op jit(solution)/shard_map/ppermute | solution.py:22
  112.1 5.1 %collective-permute-start.17 = (f32[3,16,128]{2,1,0:T(8,128)S(1)}, f32[3,16,128]{2,1,0:T(8,128)S(1)}, u32[]{:S(2)}, u32[]{:S(2)}) collective-permute-start(f32[3,16,128]{2,1,0:T(8,128)S(1)} %get-tuple-element.10), channel_id=1, source_target_pairs={{1,0},{2,1},{3,2},{4,3},{5,4},{6,5},{7,6},{0,7},{9,8},{10,9},{11,1... | collective-permute-start | bytes 73736 | tf_op jit(solution)/shard_map/ppermute | solution.py:25
  117.4 6.3 %collective-permute-start.18 = (f32[4,2,128]{2,1,0:T(2,128)S(1)}, f32[4,2,128]{2,1,0:T(2,128)S(1)}, u32[]{:S(2)}, u32[]{:S(2)}) collective-permute-start(f32[4,2,128]{2,1,0:T(2,128)S(1)} %get-tuple-element.19), channel_id=1, source_target_pairs={{0,8},{8,16},{16,24},{1,9},{9,17},{17,25},{2,10},{10,18},{18,26},{... | collective-permute-start | bytes 12296 | tf_op jit(solution)/shard_map/ppermute | solution.py:22
  122.2 5.5 %collective-permute-start.19 = (f32[4,2,128]{2,1,0:T(2,128)S(1)}, f32[4,2,128]{2,1,0:T(2,128)S(1)}, u32[]{:S(2)}, u32[]{:S(2)}) collective-permute-start(f32[4,2,128]{2,1,0:T(2,128)S(1)} %get-tuple-element.20), channel_id=1, source_target_pairs={{8,0},{16,8},{24,16},{9,1},{17,9},{25,17},{10,2},{18,10},{26,18},{... | collective-permute-start | bytes 12296 | tf_op jit(solution)/shard_map/ppermute | solution.py:25
  127.8 3.9 %copy-start.2 = (f32[80,64,32]{1,2,0:S(1)}, f32[80,64,32]{1,2,0}, u32[]{:S(2)}) copy-start(f32[80,64,32]{1,2,0} %copy-done) | copy-start | bytes 1966084
  127.8 3.9 %copy-start.4 = (f32[4,8,80,64]{3,1,0,2:T(8,128)S(1)}, f32[4,8,80,64]{3,1,0,2:T(8,128)}, u32[]{:S(2)}) copy-start(f32[4,8,80,64]{3,1,0,2:T(8,128)} %get-tuple-element.38) | copy-start | bytes 1966084
  131.7 34.0 %copy-start.3 = (f32[80,64,32]{1,2,0:S(1)}, f32[80,64,32]{1,2,0}, u32[]{:S(2)}) copy-start(f32[80,64,32]{1,2,0} %copy-done) | copy-start | bytes 1966084
